TPU v7x, 32 devices: a whole 2x2x4 slice. The times are simulated.
32 devices in a mesh: tensor: 2 (over x), dp: 16 (over z, y, core).
Axes of the slice: x: 2, y: 2, z: 4, core: 2. Of those that a mesh axis runs over, the one named last changes fastest.
Arguments:
- tokens: bfloat16 [2048, 8192], P('dp', 'tensor'), may hold values from -6 to 6
- projection_weights: bfloat16 [2, 8192, 256], P(None, None, 'tensor'), may hold values from -0.0625 to 0.0625
- head_cotangent: bfloat16 [2, 2048, 256], P(None, 'dp', 'tensor'), may hold values from -6 to 6
- frequencies: int32 [2, 1024], replicated, may hold values from 0 to 8191, as said below
- sign_bits: int32 [2, 8192], replicated, may hold values 0 or 1
- first_moment: float32 [2, 1024, 256], P(None, 'dp', 'tensor'), may hold values from -6 to 6
- second_moment: float32 [2, 1024, 256], P(None, 'dp', 'tensor'), may hold values from 0.2 to 2
Outputs:
- input_gradient: bfloat16 [2048, 8192], P('dp', 'tensor')
- new_first: float32 [2, 1024, 256], P(None, 'dp', 'tensor')
- new_second: float32 [2, 1024, 256], P(None, 'dp', 'tensor')
- full_direction: bfloat16 [2, 8192, 256], P(None, 'dp', 'tensor')
Inputs may be any that keep to these rules, and one draw needn't show every extreme that they name: Each row holds 1024 different frequencies, and 0 is one of them.
All inputs are finite; a program needn't handle non-finite values.
Results may differ from a plain program's by a relative error of at most 0.013.
Values may be sent and summed in bfloat16 or wider, within the bound.
A program may use at most 64 MiB of HBM per device.

v0:
```python
import functools
import math

import jax
import jax.numpy as jnp
from jax import lax
from jax.experimental import pallas as pl
from jax.experimental.pallas import tpu as pltpu
from jax.sharding import PartitionSpec as P

first_fix = 1.0 - 0.9**10
second_fix = 1.0 - 0.95**10
epsilon = 1e-08


def trig(phase, width):
    phase = phase % (4 * width)
    quarter = (phase + width // 2) // width
    x = (phase - quarter * width).astype(jnp.float32) * (math.pi / (2 * width))
    y = x * x
    c = 1.0 + y * (-0.5 + y * (1 / 24 + y * (-1 / 720 + y * (1 / 40320 - y * (1 / 3628800)))))
    s = x * (1.0 + y * (-1 / 6 + y * (1 / 120 + y * (-1 / 5040 + y * (1 / 362880)))))
    quarter = quarter % 4
    odd = quarter % 2 == 1
    cosine = jnp.where(odd, s, c) * jnp.where((quarter == 1) | (quarter == 2), -1.0, 1.0)
    sine = jnp.where(odd, c, s) * jnp.where(quarter >= 2, -1.0, 1.0)
    return cosine, sine


def project_kernel(low_rows, chunk, tok_ref, hc_ref, sign_ref, ca_ref, sa_ref, cb_ref, sb_ref, out_ref, acc):
    rank = acc.shape[2]
    groups = chunk // low_rows
    dp, n_tensor, _, own, cols = out_ref.shape
    acc[...] = jnp.zeros_like(acc)

    def step(h, carry):
        columns = pl.ds(pl.multiple_of(h * chunk, chunk), chunk)
        tok = tok_ref[:, columns]
        for m in range(2):
            ks = slice(m * rank, (m + 1) * rank)
            cb, sb = cb_ref[:, ks], sb_ref[:, ks]
            parts = []
            for g in range(groups):
                row = pl.ds(h * groups + g, 1)
                parts.append((ca_ref[row, ks] * cb - sa_ref[row, ks] * sb).astype(jnp.bfloat16))
            basis = jnp.concatenate(parts, axis=0) if groups > 1 else parts[0]
            signed = tok * sign_ref[pl.ds(m, 1), columns].astype(jnp.bfloat16)
            acc[m] += jnp.dot(signed, basis, preferred_element_type=jnp.float32)
        return carry

    lax.fori_loop(0, tok_ref.shape[1] // chunk, step, 0)
    for m in range(2):
        low = lax.dot_general(
            acc[m].astype(jnp.bfloat16),
            hc_ref[m],
            (((0,), (0,)), ((), ())),
            preferred_element_type=jnp.float32,
        ).astype(jnp.bfloat16)
        for t in range(n_tensor):
            out_ref[:, t, m] = low[:, t * cols : (t + 1) * cols].reshape(dp, own, cols)


def shards(
    tokens, projection_weights, head_cotangent, frequencies, sign_bits, first_moment, second_moment
):
    rows, local_width = tokens.shape
    n_tensor, n_dp = lax.axis_size("tensor"), lax.axis_size("dp")
    width = local_width * n_tensor
    token_count = rows * n_dp
    rank = frequencies.shape[1]
    own, cols = first_moment.shape[1], first_moment.shape[2]
    own_rows = projection_weights.shape[1] // n_dp
    low_rows = min(128, own_rows)
    chunk = min(256, local_width)
    me_t, me_d = lax.axis_index("tensor"), lax.axis_index("dp")
    offset = me_t * local_width
    row_offset = me_d * own_rows

    head_contract = (((1,), (1,)), ((), ()))

    def partial(t):
        total = 0.0
        for m in range(2):
            w = lax.dynamic_slice_in_dim(projection_weights[m], t * local_width, local_width, 0)
            total = total + lax.dot_general(
                head_cotangent[m], w, head_contract, preferred_element_type=jnp.float32
            )
        return total.astype(jnp.bfloat16)

    arrived = []
    for shift in range(1, n_tensor):
        sent = partial((me_t + shift) % n_tensor)
        pairs = [(i, (i + shift) % n_tensor) for i in range(n_tensor)]
        arrived.append(lax.ppermute(sent, "tensor", pairs))
    mine = partial(me_t)
    heads = lax.all_gather(head_cotangent, "tensor", axis=2, tiled=True)

    f = frequencies.reshape(1, 2 * rank)
    scale = jnp.where(f == 0, math.sqrt(1.0 / width), math.sqrt(2.0 / width)).astype(jnp.float32)
    cb, sb = trig((2 * lax.iota(jnp.int32, low_rows)[:, None] + 1) * f, width)
    hi = offset + low_rows * lax.iota(jnp.int32, local_width // low_rows)
    ca, sa = trig(2 * hi[:, None] * f, width)
    ca, sa = ca * scale, sa * scale
    hi_b = row_offset + low_rows * lax.iota(jnp.int32, own_rows // low_rows)
    ra, rb = trig(2 * hi_b[:, None] * f, width)
    ra, rb = ra * scale, rb * scale
    signs = (2 * sign_bits - 1).astype(jnp.float32)
    my_signs = lax.dynamic_slice_in_dim(signs, offset, local_width, 1)

    vmem = pl.BlockSpec(memory_space=pltpu.VMEM)
    low = pl.pallas_call(
        functools.partial(project_kernel, low_rows, chunk),
        out_shape=jax.ShapeDtypeStruct((n_dp, n_tensor, 2, own, cols), jnp.bfloat16),
        in_specs=[vmem] * 7,
        out_specs=vmem,
        scratch_shapes=[pltpu.VMEM((2, rows, rank), jnp.float32)],
        compiler_params=pltpu.CompilerParams(vmem_limit_bytes=32 * 1024 * 1024),
        cost_estimate=pl.CostEstimate(
            flops=4 * rows * local_width * rank * 4, bytes_accessed=8 * 2**20, transcendentals=0
        ),
    )(tokens, heads, my_signs, ca, sa, cb, sb)
    pieces = lax.all_to_all(
        low.reshape(n_dp * n_tensor, 2, own, cols), ("dp", "tensor"), 0, 0, tiled=True
    )
    gradient = jnp.sum(pieces.astype(jnp.float32), axis=0) / math.sqrt(token_count)
    new_first = 0.9 * first_moment + 0.1 * gradient
    new_second = 0.95 * second_moment + 0.05 * gradient * gradient
    direction = (new_first / first_fix / (jnp.sqrt(new_second / second_fix) + epsilon)).astype(
        jnp.bfloat16
    )
    gathered = lax.all_gather(direction, "dp", axis=1, tiled=True)
    back = []
    for m in range(2):
        ks = slice(m * rank, (m + 1) * rank)
        basis = ra[:, None, ks] * cb[None, :, ks] - rb[:, None, ks] * sb[None, :, ks]
        row_sign = lax.dynamic_slice_in_dim(signs[m], row_offset, own_rows, 0)[:, None]
        basis = basis.reshape(own_rows, rank).astype(jnp.bfloat16)
        product = jnp.dot(basis, gathered[m], preferred_element_type=jnp.float32)
        back.append((product * row_sign).astype(jnp.bfloat16))
    summed = mine.astype(jnp.float32)
    for piece in arrived:
        summed = summed + piece.astype(jnp.float32)
    return (summed.astype(jnp.bfloat16), new_first, new_second, jnp.stack(back))


def solution(mesh):
    in_specs = (
        P("dp", "tensor"),
        P(None, None, "tensor"),
        P(None, "dp", "tensor"),
        P(),
        P(),
        P(None, "dp", "tensor"),
        P(None, "dp", "tensor"),
    )
    out_specs = (
        P("dp", "tensor"),
        P(None, "dp", "tensor"),
        P(None, "dp", "tensor"),
        P(None, "dp", "tensor"),
    )
    return jax.shard_map(shards, mesh=mesh, in_specs=in_specs, out_specs=out_specs, check_vma=False)
```

profile of v0, /device:TPU:0, one launch (start us, length us, event | category | flops | bytes accessed | tf_op | source)
XLA Modules:
  0.0 105.2 jit_solution(16596995826020222319)
XLA Ops:
  0.7 3.8 %fusion.57 = (bf16[1,8192,128]{2,1,0:T(8,128)(2,1)S(1)}, bf16[1,8192,128]{2,1,0:T(8,128)(2,1)}) fusion(bf16[2,8192,128]{2,1,0:T(8,128)(2,1)} %param.8), kind=kLoop, calls=%fused_computation.147 | loop fusion | bytes 8388608 | tf_op jit(solution)/shard_map/slice | solution.py:84
  4.5 0.0 copy-done.5
  4.5 2.4 %fusion.15 = f32[4096,128]{1,0:T(8,128)S(1)} fusion(bf16[1,8192,128]{2,1,0:T(8,128)(2,1)} %get-tuple-element.12, s32[]{:T(128)S(6)} %select_n.130, bf16[2,128,128]{2,1,0:T(8,128)(2,1)S(1)} %copy-done.5), kind=kOutput, calls=%fused_computation.38 | convolution fusion | flops 134217728 | bytes 3178500 | tf_op jit(solution)/shard_map/dot_general | solution.py:85
  6.9 0.0 copy-start.9
  6.9 0.0 copy-start.6
  6.9 1.4 %fusion.4 = bf16[128,4096]{0,1:T(8,128)(2,1)} fusion(f32[4096,128]{1,0:T(8,128)S(1)} %fusion.15, bf16[1,8192,128]{2,1,0:T(8,128)(2,1)S(1)} %get-tuple-element.11, s32[]{:T(128)S(6)} %select_n.130, bf16[2,128,128]{2,1,0:T(8,128)(2,1)S(1)} %copy-done.5), kind=kOutput, calls=%fused_computation.6 | convolution fusion | flops 135266304 | bytes 4227076 | tf_op jit(solution)/shard_map/dot_general | solution.py:85
  8.4 3.0 %collective-permute-start = (bf16[128,4096]{0,1:T(8,128)(2,1)}, bf16[128,4096]{0,1:T(8,128)(2,1)}, u32[]{:S(2)}, u32[]{:S(2)}) collective-permute-start(bf16[128,4096]{0,1:T(8,128)(2,1)} %fusion.4), channel_id=1, source_target_pairs={{0,16},{16,0},{1,17},{17,1},{2,18},{18,2},{3,19},{19,3},{4,20},{20... | collective-permute-start | bytes 3145736 | tf_op jit(solution)/shard_map/ppermute | solution.py:94
  11.3 24.8 %all_gather.6.hc_ref = bf16[2,128,256]{2,1,0:T(8,128)(2,1)S(1)} all-gather(bf16[2,128,128]{2,1,0:T(8,128)(2,1)S(1)} %copy-done.5), channel_id=1, replica_groups=mesh['tensor'=2,'dp'=16] {'tensor'}, dimensions={2}, use_global_device_ids=true | all-gather | bytes 196608 | tf_op jit(solution)/shard_map/all_gather | solution.py:96
  36.2 3.0 %select_multiply_fusion = (f32[128,2048]{1,0:T(8,128)S(1)}, f32[128,2048]{1,0:T(8,128)S(1)}) fusion(s32[2048]{0:T(1024)S(1)} %bitcast.55, s32[128]{0:T(128)S(1)} %multiply_add_fusion.5), kind=kLoop, calls=%fused_computation.43 | loop fusion | flops 22282240 | bytes 2105856 | tf_op jit(solution)/shard_map/mul | solution.py:26
  39.2 0.8 multiply_multiply_fusion.2
  40.0 9.4 %shard_map.102 = bf16[16,2,2,64,128]{4,3,2,1,0:T(8,128)(2,1)} custom-call(bf16[128,4096]{1,0:T(8,128)(2,1)S(1)} %copy-done, bf16[2,128,256]{2,1,0:T(8,128)(2,1)S(1)} %all_gather.6.hc_ref, f32[2,4096]{1,0:T(2,128)S(1)} %constant_dynamic-slice_fusion.2.sign_ref, f32[32,2048]{1,0:T(8,128)S(1)} %get-tuple-element.26.ca_ref, ...), custom_call_target="tpu_custom_call" | custom-call | flops 8589934592 | bytes 8388608 | tf_op jit(solution)/shard_map/pallas_call | solution.py:111
  49.5 6.1 %all-to-all-start = ((bf16[32,2,64,128]{3,2,1,0:T(8,128)(2,1)}), bf16[32,2,64,128]{3,2,1,0:T(8,128)(2,1)S(1)}, u32[]{:S(2)}, u32[]{:S(2)}) async-start(bf16[32,2,64,128]{3,2,1,0:T(8,128)(2,1)} %bitcast.8), calls=%async_computation | async-start | bytes 2097152 | tf_op jit(solution)/shard_map/all_to_all | solution.py:122
  55.6 3.0 %fusion.20 = f32[4096,128]{1,0:T(8,128)} fusion(bf16[1,8192,128]{2,1,0:T(8,128)(2,1)} %get-tuple-element.12, s32[]{:T(128)S(6)} %select_n.128, bf16[2,128,128]{2,1,0:T(8,128)(2,1)S(1)} %copy-done.5), kind=kOutput, calls=%fused_computation.41 | convolution fusion | flops 134217728 | bytes 3178500 | tf_op jit(solution)/shard_map/dot_general | solution.py:85
  58.6 0.1 fusion.60
  58.7 0.3 multiply_multiply_fusion.7
  59.0 0.2 fusion.58
  59.3 0.3 subtract_convert_fusion
  59.6 1.3 %subtract_convert_fusion.1 = bf16[4,128,1024]{2,1,0:T(8,128)(2,1)} fusion(f32[128,1024]{1,0:T(8,128)S(1)} %get-tuple-element.30, f32[4,1024]{1,0:T(4,128)S(1)} %get-tuple-element.32, f32[128,1024]{1,0:T(8,128)S(1)} %get-tuple-element.13, f32[4,1024]{1,0:T(4,128)S(1)} %get-tuple-element.19), kind=kLoop, calls=%fused_computation.8 | loop fusion | flops 2097152 | bytes 2129920 | tf_op jit(solution)/shard_map/convert_element_type | solution.py:137
  60.8 0.0 collective-permute-done
  60.8 0.0 copy-done.1
  60.8 1.0 copy-done.3
  61.8 1.7 %add_convert_fusion = bf16[128,4096]{0,1:T(8,128)(2,1)S(1)} fusion(bf16[128,4096]{0,1:T(8,128)(2,1)} %collective-permute-done, f32[4096,128]{1,0:T(8,128)S(1)} %copy-done.1, bf16[1,8192,128]{2,1,0:T(8,128)(2,1)S(1)} %copy-done.3, s32[]{:T(128)S(6)} %select_n.128, bf16[2,128,128]{2,1,0:T(8,128)(2,1)S(1)} %copy-done.5), kind=kOutput, calls=%fused_computation.10 | convolution fusion | flops 137363456 | bytes 5275652 | tf_op jit(solution)/shard_map/dot_general | solution.py:85
  63.5 0.0 copy-start.7
  63.5 0.0 copy-start.8
  63.6 1.3 %copy.11 = bf16[128,4096]{1,0:T(8,128)(2,1)} copy(bf16[128,4096]{0,1:T(8,128)(2,1)S(1)} %add_convert_fusion) | data formatting | bytes 2097152
  64.9 16.9 %all-to-all-done = bf16[32,2,64,128]{3,2,1,0:T(8,128)(2,1)S(1)} async-done(((bf16[32,2,64,128]{3,2,1,0:T(8,128)(2,1)}), bf16[32,2,64,128]{3,2,1,0:T(8,128)(2,1)S(1)}, u32[]{:S(2)}, u32[]{:S(2)}) %all-to-all-start) | async-done | bytes 1048608 | tf_op jit(solution)/shard_map/all_to_all | solution.py:122
  81.8 0.2 convert_reduce_fusion
  82.0 0.7 divide_convert_fusion
  82.7 20.9 %all_gather.7 = bf16[2,1024,128]{2,1,0:T(8,128)(2,1)S(1)} all-gather(bf16[2,64,128]{2,1,0:T(8,128)(2,1)S(1)} %get-tuple-element.8), channel_id=1, replica_groups=mesh['tensor'=2,'dp'=16] {'dp'}, dimensions={1}, use_global_device_ids=true | all-gather | bytes 557056 | tf_op jit(solution)/shard_map/all_gather | solution.py:131
  103.5 0.4 fusion.7
  104.0 0.4 fusion.8
  104.4 0.7 pad_maximum_fusion
  (22 shorter events, 0.1 us)
Async XLA Ops:
  0.6 3.9 %copy-start.5 = (bf16[2,128,128]{2,1,0:T(8,128)(2,1)S(1)}, bf16[2,128,128]{2,1,0:T(8,128)(2,1)}, u32[]{:S(2)}) copy-start(bf16[2,128,128]{2,1,0:T(8,128)(2,1)} %param.9) | copy-start | bytes 196612
  4.5 3.9 %copy-start.2 = (bf16[1,8192,128]{2,1,0:T(8,128)(2,1)}, bf16[1,8192,128]{2,1,0:T(8,128)(2,1)S(1)}, u32[]{:S(2)}) copy-start(bf16[1,8192,128]{2,1,0:T(8,128)(2,1)S(1)} %get-tuple-element.11) | copy-start | bytes 6291460
  6.9 29.2 %copy-start.9 = (s32[2,1024]{1,0:T(2,128)S(1)}, s32[2,1024]{1,0:T(2,128)}, u32[]{:S(2)}) copy-start(s32[2,1024]{1,0:T(2,128)} %param.10) | copy-start | bytes 24580
  6.9 29.2 %copy-start.6 = (s32[2,8192]{1,0:T(2,128)S(1)}, s32[2,8192]{1,0:T(2,128)}, u32[]{:S(2)}) copy-start(s32[2,8192]{1,0:T(2,128)} %param.11) | copy-start | bytes 196612
  8.4 31.7 %copy-start = (bf16[128,4096]{1,0:T(8,128)(2,1)S(1)}, bf16[128,4096]{1,0:T(8,128)(2,1)}, u32[]{:S(2)}) copy-start(bf16[128,4096]{1,0:T(8,128)(2,1)} %tok_ref.1) | copy-start | bytes 3145732
  8.4 52.5 %collective-permute-start = (bf16[128,4096]{0,1:T(8,128)(2,1)}, bf16[128,4096]{0,1:T(8,128)(2,1)}, u32[]{:S(2)}, u32[]{:S(2)}) collective-permute-start(bf16[128,4096]{0,1:T(8,128)(2,1)} %fusion.4), channel_id=1, source_target_pairs={{0,16},{16,0},{1,17},{17,1},{2,18},{18,2},{3,19},{19,3},{4,20},{20... | collective-permute-start | bytes 3145736 | tf_op jit(solution)/shard_map/ppermute | solution.py:94
  49.5 32.3 %all-to-all-start = ((bf16[32,2,64,128]{3,2,1,0:T(8,128)(2,1)}), bf16[32,2,64,128]{3,2,1,0:T(8,128)(2,1)S(1)}, u32[]{:S(2)}, u32[]{:S(2)}) async-start(bf16[32,2,64,128]{3,2,1,0:T(8,128)(2,1)} %bitcast.8), calls=%async_computation | async-start | bytes 2097152 | tf_op jit(solution)/shard_map/all_to_all | solution.py:122
  59.2 1.6 %copy-start.1 = (f32[4096,128]{1,0:T(8,128)S(1)}, f32[4096,128]{1,0:T(8,128)}, u32[]{:S(2)}) copy-start(f32[4096,128]{1,0:T(8,128)} %fusion.20) | copy-start | bytes 6291460
  59.2 2.6 %copy-start.3 = (bf16[1,8192,128]{2,1,0:T(8,128)(2,1)S(1)}, bf16[1,8192,128]{2,1,0:T(8,128)(2,1)}, u32[]{:S(2)}) copy-start(bf16[1,8192,128]{2,1,0:T(8,128)(2,1)} %copy-done.2) | copy-start | bytes 6291460
  63.5 18.4 %copy-start.7 = (f32[2,64,128]{2,1,0:T(8,128)S(1)}, f32[2,64,128]{2,1,0:T(8,128)}, u32[]{:S(2)}) copy-start(f32[2,64,128]{2,1,0:T(8,128)} %param.13) | copy-start | bytes 196612
  63.5 18.4 %copy-start.8 = (f32[2,64,128]{2,1,0:T(8,128)S(1)}, f32[2,64,128]{2,1,0:T(8,128)}, u32[]{:S(2)}) copy-start(f32[2,64,128]{2,1,0:T(8,128)} %param.12) | copy-start | bytes 196612
  64.9 39.1 %copy-start.4 = (bf16[4,128,1024]{2,1,0:T(8,128)(2,1)S(1)}, bf16[4,128,1024]{2,1,0:T(8,128)(2,1)}, u32[]{:S(2)}) copy-start(bf16[4,128,1024]{2,1,0:T(8,128)(2,1)} %subtract_convert_fusion.1) | copy-start | bytes 3145732
where the time goes:
time: 106 us; the launch traced here: 105 us
  blocking collectives  45.7 us (43%)
  waiting for transfers between devices  16.9 us (16%)
  Pallas kernels  9.44 us (9%)
  matrix products  9.42 us (9%)
  starting transfers between devices  9.07 us (9%)
  other arithmetic  7.25 us (7%)
  local copies, waits for them, and re-layouts  6.54 us (6%)
    all_gather x1, blocking collectives, shards(): heads = lax.all_gather(head_cotangent, 'tensor', axis=2, tiled=True)  24.8 us
    all_gather x1, blocking collectives, shards(): gathered = lax.all_gather(direction, 'dp', axis=1, tiled=True)  20.9 us
    all_to_all x1, waiting for transfers between devices, shards(): lax.all_to_all(low.reshape(n_dp * n_tensor, 2, own, cols), ('dp', 'tensor...  16.9 us
    pallas_call x1, Pallas kernels, shards(): pl.pallas_call(functools.partial(project_kernel, low_rows, chunk), out_sh...  9.44 us
    dot_general x4, matrix products, partial(): lax.dot_general(head_cotangent[m], w, head_contract, preferred_element_ty...  8.54 us
    all_to_all x1, starting transfers between devices, shards(): lax.all_to_all(low.reshape(n_dp * n_tensor, 2, own, cols), ('dp', 'tensor...  6.1 us
    slice x1, local copies, waits for them, and re-layouts, partial(): projection_weights[m]  3.84 us
    mul x1, other arithmetic, trig(): sine = jnp.where(odd, c, s) * jnp.where(quarter >= 2, -1.0, 1.0)  2.97 us
  transfers between devices with their start and end apart: 2, of which 1 were waited for; matrix products, arithmetic and copies ran while one was open for 11% of the time, Pallas kernels for 9%

commit v1 on v0

v1 whole, which is shorter than its diff:
```python
import functools
import math

import jax
import jax.numpy as jnp
from jax import lax
from jax.experimental import pallas as pl
from jax.experimental.pallas import tpu as pltpu
from jax.sharding import PartitionSpec as P

first_fix = 1.0 - 0.9**10
second_fix = 1.0 - 0.95**10
epsilon = 1e-08


def trig(phase, width):
    phase = phase % (4 * width)
    quarter = (phase + width // 2) // width
    x = (phase - quarter * width).astype(jnp.float32) * (math.pi / (2 * width))
    y = x * x
    c = 1.0 + y * (-0.5 + y * (1 / 24 + y * (-1 / 720 + y * (1 / 40320 - y * (1 / 3628800)))))
    s = x * (1.0 + y * (-1 / 6 + y * (1 / 120 + y * (-1 / 5040 + y * (1 / 362880)))))
    quarter = quarter % 4
    odd = quarter % 2 == 1
    cosine = jnp.where(odd, s, c) * jnp.where((quarter == 1) | (quarter == 2), -1.0, 1.0)
    sine = jnp.where(odd, c, s) * jnp.where(quarter >= 2, -1.0, 1.0)
    return cosine, sine


def step_kernel(
    low_rows, chunk, token_count,
    tok_ref, w_ref, hc_ref, sign_ref, back_sign_ref, ca_ref, sa_ref, cb_ref, sb_ref, ra_ref, rb_ref,
    first_ref, second_ref,
    grad_ref, new_first_ref, new_second_ref, full_ref,
    acc, hc_all, tg_send, tg_recv, low_send, low_recv, part, x_send, x_recv, dirs, back_basis,
    hc_sems, tg_sems, low_sems, x_sems, dir_sems,
):
    rank = acc.shape[2]
    rows, lw = tok_ref.shape
    groups = chunk // low_rows
    n_dp, n_t, _, own, cols = low_send.shape
    me_t, me_d = lax.axis_index("tensor"), lax.axis_index("dp")

    def remote(src, dst, sems, slot, tensor, dp):
        return pltpu.make_async_remote_copy(
            src_ref=src,
            dst_ref=dst,
            send_sem=sems.at[0, slot],
            recv_sem=sems.at[1, slot],
            device_id={"tensor": tensor, "dp": dp},
            device_id_type=pl.DeviceIdType.MESH,
        )

    def peer_t(s):
        return lax.rem(me_t + s, n_t)

    def peer_d(s):
        return lax.rem(me_d + s, n_dp)

    barrier = pltpu.get_barrier_semaphore()

    def greet_t(s, carry):
        pl.semaphore_signal(
            barrier, inc=1, device_id={"tensor": peer_t(s), "dp": me_d},
            device_id_type=pl.DeviceIdType.MESH,
        )
        return carry

    def greet_d(s, carry):
        pl.semaphore_signal(
            barrier, inc=1, device_id={"tensor": me_t, "dp": peer_d(s)},
            device_id_type=pl.DeviceIdType.MESH,
        )
        return carry

    lax.fori_loop(1, n_t, greet_t, 0)
    lax.fori_loop(1, n_dp, greet_d, 0)
    pl.semaphore_wait(barrier, n_t + n_dp - 2)

    def hc_copy(s):
        return remote(hc_ref, hc_all.at[me_t], hc_sems, s, peer_t(s), me_d)

    def tg_copy(s):
        return remote(tg_send.at[s - 1], tg_recv.at[s - 1], tg_sems, s, peer_t(s), me_d)

    def low_copy(s):
        return remote(low_send.at[peer_d(s)], low_recv.at[s - 1], low_sems, s, me_t, peer_d(s))

    def x_copy(s):
        return remote(x_send.at[peer_t(s)], x_recv.at[s - 1], x_sems, s, peer_t(s), me_d)

    def dir_copy(s):
        return remote(dirs.at[me_d], dirs.at[me_d], dir_sems, s, me_t, peer_d(s))

    def each(count, act):
        def body(s, carry):
            act(s)
            return carry

        lax.fori_loop(1, count, body, 0)

    each(n_t, lambda s: hc_copy(s).start())
    hc_all[pl.ds(me_t, 1)] = hc_ref[...][None]
    wide = min(512, lw)

    def partial(t, j):
        total = 0.0
        for m in range(2):
            w = w_ref[m, pl.ds(pl.multiple_of(t * lw + j * wide, wide), wide), :]
            total = total + lax.dot_general(
                hc_ref[m], w, (((1,), (1,)), ((), ())), preferred_element_type=jnp.float32
            )
        return total.astype(jnp.bfloat16)

    def send_half(s):
        def tile(j, carry):
            tg_send[s - 1, :, pl.ds(pl.multiple_of(j * wide, wide), wide)] = partial(peer_t(s), j)
            return carry

        lax.fori_loop(0, lw // wide, tile, 0)
        tg_copy(s).start()

    each(n_t, send_half)
    acc[...] = jnp.zeros_like(acc)

    def tables(a_ref, b_ref, row, ks):
        row = pl.ds(row, 1)
        return (a_ref[row, ks] * cb_ref[:, ks] - b_ref[row, ks] * sb_ref[:, ks]).astype(jnp.bfloat16)

    def step(h, carry):
        columns = pl.ds(pl.multiple_of(h * chunk, chunk), chunk)
        tok = tok_ref[:, columns]
        for m in range(2):
            ks = slice(m * rank, (m + 1) * rank)
            parts = [tables(ca_ref, sa_ref, h * groups + g, ks) for g in range(groups)]
            basis = jnp.concatenate(parts, axis=0) if groups > 1 else parts[0]
            signed = tok * sign_ref[pl.ds(m, 1), columns].astype(jnp.bfloat16)
            acc[m] += jnp.dot(signed, basis, preferred_element_type=jnp.float32)
        return carry

    lax.fori_loop(0, lw // chunk, step, 0)
    each(n_t, lambda s: hc_copy(s).wait_recv())
    for m in range(2):
        heads = jnp.concatenate([hc_all[t, m] for t in range(n_t)], axis=1)
        low = lax.dot_general(
            acc[m].astype(jnp.bfloat16),
            heads,
            (((0,), (0,)), ((), ())),
            preferred_element_type=jnp.float32,
        ).astype(jnp.bfloat16)
        for t in range(n_t):
            low_send[:, t, m] = low[:, t * cols : (t + 1) * cols].reshape(n_dp, own, cols)
    each(n_dp, lambda s: low_copy(s).start())

    def own_tile(j, carry):
        grad_ref[:, pl.ds(pl.multiple_of(j * wide, wide), wide)] = partial(me_t, j)
        return carry

    lax.fori_loop(0, lw // wide, own_tile, 0)

    def back_rows(h, carry):
        for m in range(2):
            ks = slice(m * rank, (m + 1) * rank)
            place = pl.ds(pl.multiple_of(h * low_rows, low_rows), low_rows)
            back_basis[m, place, :] = tables(ra_ref, rb_ref, h, ks)
        return carry

    lax.fori_loop(0, back_basis.shape[1] // low_rows, back_rows, 0)
    part[...] = low_send[pl.ds(me_d, 1)][0].astype(jnp.float32)

    def add(s):
        low_copy(s).wait_recv()
        part[...] += low_recv[pl.ds(s - 1, 1)][0].astype(jnp.float32)

    each(n_dp, add)
    x_send[...] = part[...].astype(jnp.bfloat16)
    each(n_t, lambda s: x_copy(s).start())
    total = part[pl.ds(me_t, 1)][0]
    each(n_t, lambda s: x_copy(s).wait_recv())
    for s in range(1, n_t):
        total = total + x_recv[s - 1].astype(jnp.float32)
    gradient = total / math.sqrt(token_count)
    new_first = 0.9 * first_ref[...] + 0.1 * gradient
    new_second = 0.95 * second_ref[...] + 0.05 * gradient * gradient
    direction = new_first / first_fix / (jnp.sqrt(new_second / second_fix) + epsilon)
    dirs[pl.ds(me_d, 1)] = direction.astype(jnp.bfloat16)[None]
    each(n_dp, lambda s: dir_copy(s).start())
    new_first_ref[...] = new_first
    new_second_ref[...] = new_second
    each(n_t, lambda s: tg_copy(s).wait_recv())

    def finish(j, carry):
        place = pl.ds(pl.multiple_of(j * wide, wide), wide)
        summed = grad_ref[:, place].astype(jnp.float32)
        for s in range(1, n_t):
            summed = summed + tg_recv[s - 1, :, place].astype(jnp.float32)
        grad_ref[:, place] = summed.astype(jnp.bfloat16)
        return carry

    lax.fori_loop(0, lw // wide, finish, 0)

    def dir_arrival(s):
        source = lax.rem(me_d + n_dp - s, n_dp)
        remote(dirs.at[source], dirs.at[source], dir_sems, s, me_t, source).wait_recv()

    each(n_dp, dir_arrival)
    for m in range(2):
        product = jnp.dot(
            back_basis[m],
            dirs[:, m].reshape(rank, cols),
            preferred_element_type=jnp.float32,
        )
        full_ref[m] = (product * back_sign_ref[m]).astype(jnp.bfloat16)
    each(n_t, lambda s: hc_copy(s).wait_send())
    each(n_t, lambda s: tg_copy(s).wait_send())
    each(n_dp, lambda s: low_copy(s).wait_send())
    each(n_t, lambda s: x_copy(s).wait_send())
    each(n_dp, lambda s: dir_copy(s).wait_send())


def shards(
    tokens, projection_weights, head_cotangent, frequencies, sign_bits, first_moment, second_moment
):
    rows, local_width = tokens.shape
    n_tensor, n_dp = lax.axis_size("tensor"), lax.axis_size("dp")
    width = local_width * n_tensor
    token_count = rows * n_dp
    rank = frequencies.shape[1]
    own, cols = first_moment.shape[1], first_moment.shape[2]
    own_rows = projection_weights.shape[1] // n_dp
    low_rows = min(128, own_rows)
    chunk = min(256, local_width)
    me_t, me_d = lax.axis_index("tensor"), lax.axis_index("dp")
    offset = me_t * local_width
    row_offset = me_d * own_rows

    f = frequencies.reshape(1, 2 * rank)
    scale = jnp.where(f == 0, math.sqrt(1.0 / width), math.sqrt(2.0 / width)).astype(jnp.float32)
    cb, sb = trig((2 * lax.iota(jnp.int32, low_rows)[:, None] + 1) * f, width)
    hi = offset + low_rows * lax.iota(jnp.int32, local_width // low_rows)
    ca, sa = trig(2 * hi[:, None] * f, width)
    ca, sa = ca * scale, sa * scale
    hi_b = row_offset + low_rows * lax.iota(jnp.int32, own_rows // low_rows)
    ra, rb = trig(2 * hi_b[:, None] * f, width)
    ra, rb = ra * scale, rb * scale
    signs = (2 * sign_bits - 1).astype(jnp.float32)
    my_signs = lax.dynamic_slice_in_dim(signs, offset, local_width, 1)

    back_signs = lax.dynamic_slice_in_dim(signs, row_offset, own_rows, 1)[:, :, None]
    back_signs = jnp.broadcast_to(back_signs, (2, own_rows, cols))

    vmem = pl.BlockSpec(memory_space=pltpu.VMEM)
    bf16, f32 = jnp.bfloat16, jnp.float32
    pair = pltpu.SemaphoreType.DMA
    return pl.pallas_call(
        functools.partial(step_kernel, low_rows, chunk, token_count),
        out_shape=(
            jax.ShapeDtypeStruct((rows, local_width), bf16),
            jax.ShapeDtypeStruct((2, own, cols), f32),
            jax.ShapeDtypeStruct((2, own, cols), f32),
            jax.ShapeDtypeStruct((2, own_rows, cols), bf16),
        ),
        in_specs=[vmem] * 13,
        out_specs=(vmem,) * 4,
        scratch_shapes=[
            pltpu.VMEM((2, rows, rank), f32),
            pltpu.VMEM((n_tensor, 2, rows, cols), bf16),
            pltpu.VMEM((n_tensor - 1, rows, local_width), bf16),
            pltpu.VMEM((n_tensor - 1, rows, local_width), bf16),
            pltpu.VMEM((n_dp, n_tensor, 2, own, cols), bf16),
            pltpu.VMEM((n_dp - 1, n_tensor, 2, own, cols), bf16),
            pltpu.VMEM((n_tensor, 2, own, cols), f32),
            pltpu.VMEM((n_tensor, 2, own, cols), bf16),
            pltpu.VMEM((n_tensor - 1, 2, own, cols), bf16),
            pltpu.VMEM((n_dp, 2, own, cols), bf16),
            pltpu.VMEM((2, own_rows, rank), bf16),
            pair((2, n_tensor)),
            pair((2, n_tensor)),
            pair((2, n_dp)),
            pair((2, n_tensor)),
            pair((2, n_dp)),
        ],
        compiler_params=pltpu.CompilerParams(
            collective_id=0, has_side_effects=True, vmem_limit_bytes=56 * 1024 * 1024
        ),
    )(
        tokens, projection_weights, head_cotangent, my_signs, back_signs,
        ca, sa, cb, sb, ra, rb, first_moment, second_moment,
    )


def solution(mesh):
    in_specs = (
        P("dp", "tensor"),
        P(None, None, "tensor"),
        P(None, "dp", "tensor"),
        P(),
        P(),
        P(None, "dp", "tensor"),
        P(None, "dp", "tensor"),
    )
    out_specs = (
        P("dp", "tensor"),
        P(None, "dp", "tensor"),
        P(None, "dp", "tensor"),
        P(None, "dp", "tensor"),
    )
    return jax.shard_map(shards, mesh=mesh, in_specs=in_specs, out_specs=out_specs, check_vma=False)
```

time: 106 us -> 82.1 us (0.77)
  the two profiles are of different devices: /device:TPU:0 before, /device:TPU:21 now
where the time goes in v1:
time: 82.1 us; the launch traced here: 81.7 us
  Pallas kernels  63.7 us (78%)
  local copies, waits for them, and re-layouts  9.23 us (11%)
  other arithmetic  8.11 us (10%)
    pallas_call x1, Pallas kernels, shards(): pl.pallas_call(functools.partial(step_kernel, low_rows, chunk, token_coun...  63.7 us
    unnamed x5, local copies, waits for them, and re-layouts  7.6 us
    mul x1, other arithmetic, trig(): sine = jnp.where(odd, c, s) * jnp.where(quarter >= 2, -1.0, 1.0)  4.03 us

profile of v1, /device:TPU:21, one launch (start us, length us, event | category | flops | bytes accessed | tf_op | source)
XLA Modules:
  0.0 81.7 jit_solution(5975882051747256467)
XLA Ops:
  0.7 0.7 compare_select_fusion
  1.4 0.7 copy.15
  2.1 0.9 %multiply_multiply_fusion.6 = (f32[4,2048]{1,0:T(4,128)}, f32[4,2048]{1,0:T(4,128)}) fusion(f32[2048]{0:T(1024)S(1)} %compare_select_fusion, s32[2048]{0:T(1024)S(1)} %bitcast.6, s32[4]{0:T(128)S(1)} %add_multiply_fusion.3), kind=kLoop, calls=%fused_computation.83 | loop fusion | flops 712704 | bytes 81936 | tf_op jit(solution)/shard_map/mul | solution.py:245
  3.0 0.9 %add_convert_fusion = f32[2,8192]{1,0:T(2,128)S(1)} fusion(s32[2,8192]{1,0:T(2,128)} %param.11), kind=kLoop, calls=%fused_computation.62 | loop fusion | flops 49152 | bytes 131072 | tf_op jit(solution)/shard_map/convert_element_type | solution.py:246
  3.9 0.6 constant_dynamic-slice_fusion.1.sign_ref
  4.5 1.6 %multiply_multiply_fusion.2 = (f32[32,2048]{1,0:T(8,128)}, f32[32,2048]{1,0:T(8,128)}) fusion(f32[2048]{0:T(1024)S(1)} %compare_select_fusion, s32[2048]{0:T(1024)S(1)} %bitcast.7, s32[32]{0:T(128)S(1)} %add_multiply_fusion.4), kind=kLoop, calls=%fused_computation.51 | loop fusion | flops 5701632 | bytes 540800 | tf_op jit(solution)/shard_map/mul | solution.py:242
  6.1 1.0 %broadcast_in_dim.41.back_sign_ref = f32[2,512,128]{2,1,0:T(8,128)} broadcast(f32[2,512]{1,0:T(2,128)S(1)} %constant_dynamic-slice_fusion), dimensions={0,1} | broadcast | bytes 528384 | tf_op jit(solution)/shard_map/broadcast_in_dim | solution.py:250
  7.1 4.0 %select_multiply_fusion = (f32[128,2048]{1,0:T(8,128)}, f32[128,2048]{1,0:T(8,128)}) fusion(s32[2048]{0:T(1024)S(1)} %bitcast.8, s32[128]{0:T(128)S(1)} %multiply_add_fusion.3), kind=kLoop, calls=%fused_computation.20 | loop fusion | flops 22282240 | bytes 2105856 | tf_op jit(solution)/shard_map/mul | solution.py:26
  11.1 63.7 %shard_map.102 = (bf16[128,4096]{1,0:T(8,128)(2,1)}, f32[2,64,128]{2,1,0:T(8,128)}, f32[2,64,128]{2,1,0:T(8,128)}, bf16[2,512,128]{2,1,0:T(8,128)(2,1)}) custom-call(bf16[128,4096]{1,0:T(8,128)(2,1)} %tok_ref.1, bf16[2,8192,128]{2,1,0:T(8,128)(2,1)} %w_ref.1, bf16[2,128,128]{2,1,0:T(8,128)(2,1)} %hc_ref.1, f32[2,4096]{1,0:T(2,128)} %constant_dynamic-slice_fusion.1.sign_ref, ...), custom_call_target="tpu_custom_call" | custom-call | tf_op jit(solution)/shard_map/pallas_call | solution.py:255
  74.8 2.3 %copy.20 = bf16[128,4096]{1,0:T(8,128)(2,1)} copy(bf16[128,4096]{1,0:T(8,128)(2,1)} %get-tuple-element.14) | data formatting | bytes 2097152
  77.1 1.5 %copy.21 = f32[2,64,128]{2,1,0:T(8,128)} copy(f32[2,64,128]{2,1,0:T(8,128)} %get-tuple-element.15) | data formatting | bytes 131072
  78.6 1.5 %copy.22 = f32[2,64,128]{2,1,0:T(8,128)} copy(f32[2,64,128]{2,1,0:T(8,128)} %get-tuple-element.16) | data formatting | bytes 131072
  80.0 1.7 %copy.23 = bf16[2,512,128]{2,1,0:T(8,128)(2,1)} copy(bf16[2,512,128]{2,1,0:T(8,128)(2,1)} %get-tuple-element.17) | data formatting | bytes 524288
  (4 shorter events, 0.0 us)
